TPU v7x, 32 devices: a whole 2x2x4 slice. The times are simulated.
32 devices in a mesh: grp: 2 (over y), gy: 4 (over z), gx: 2 (over x), gz: 2 (over core).
Axes of the slice: x: 2, y: 2, z: 4, core: 2. Of those that a mesh axis runs over, the one named last changes fastest.
Arguments:
- pair: bfloat16 [1024, 512, 128], P(('grp', 'gx', 'gz'), 'gy'), parts along dimension 0, may hold values from -6 to 6
- lengths: int32 [2], P('grp'), parts along dimension 0, may hold values from 256 to 512
- ln_gain: float32 [128], replicated, may hold values from 0.1 to 1.9
- ln_bias: float32 [128], replicated, may hold values from -3 to 3
- w_ab: bfloat16 [128, 512], replicated, may hold values from -0.5 to 0.5
- w_gate: bfloat16 [128, 128], replicated, may hold values from -0.5 to 0.5
- out_gain: float32 [128], replicated, may hold values from 0.1 to 1.9
- out_bias: float32 [128], replicated, may hold values from -3 to 3
- w_out: bfloat16 [128, 128], replicated, may hold values from -0.5 to 0.5
Outputs:
- update: bfloat16 [1024, 512, 128], P(('grp', 'gx', 'gz'), 'gy'), parts along dimension 0
There are 2 independent parts, one for each index of `grp`. A program takes and returns all parts, laid end to end along the dimension named above; an argument that names none is the same for every part. Nothing has to cross between parts.
Inputs may be any that keep to these rules, and one draw needn't show every extreme that they name: Residues from lengths[0] on are padding.
All inputs are finite; a program needn't handle non-finite values.
Results may differ from a plain program's by a relative error of at most 0.0052.
Values may be sent and summed in bfloat16 or wider, within the bound.
A program may use at most 128 MiB of HBM per device.

v0:
```python
import jax
import jax.numpy as jnp
from jax import lax
from jax.sharding import PartitionSpec as P


def layer_norm(values, gain, bias):
    values = values.astype(jnp.float32)
    mean = jnp.mean(values, -1, keepdims=True)
    spread = jnp.mean(jnp.square(values - mean), -1, keepdims=True)
    return (values - mean) * lax.rsqrt(spread + 1e-05) * gain + bias


def channel_norm(values, gain, bias):
    mean = jnp.mean(values, 0, keepdims=True)
    spread = jnp.mean(jnp.square(values - mean), 0, keepdims=True)
    return (values - mean) * lax.rsqrt(spread + 1e-05) * gain[:, None, None] + bias[:, None, None]


def body(pair, lengths, ln_gain, ln_bias, w_ab, w_gate, out_gain, out_bias, w_out):
    tile_rows, tile_cols, width = pair.shape
    hidden = w_out.shape[0]
    row_start = lax.axis_index(("gx", "gz")) * tile_rows
    col_index = lax.axis_index("gy")
    col_start = col_index * tile_cols
    normed = layer_norm(pair, ln_gain, ln_bias).astype(jnp.bfloat16)
    flat = normed.reshape(tile_rows * tile_cols, width)
    proj = jnp.dot(flat, w_ab, preferred_element_type=jnp.float32).reshape(
        tile_rows, tile_cols, 4 * hidden
    )
    row_live = (row_start + jnp.arange(tile_rows, dtype=jnp.int32) < lengths[0]).astype(jnp.float32)
    col_live = (col_start + jnp.arange(tile_cols, dtype=jnp.int32) < lengths[0]).astype(jnp.float32)
    pair_mask = (row_live[:, None] * col_live[None, :])[..., None]
    left = (pair_mask * jax.nn.sigmoid(proj[..., :hidden]) * proj[..., hidden : 2 * hidden]).astype(
        jnp.bfloat16
    )
    right = (
        pair_mask * jax.nn.sigmoid(proj[..., 2 * hidden : 3 * hidden]) * proj[..., 3 * hidden :]
    ).astype(jnp.bfloat16)
    left_major = jnp.transpose(left, (2, 0, 1))
    right_major = jnp.transpose(right, (2, 0, 1))
    column_rows = lax.all_gather(right_major, ("gx", "gz"), axis=1, tiled=True)
    right_mine = lax.all_to_all(column_rows, "gy", split_axis=1, concat_axis=2, tiled=True)
    triangle = jnp.einsum(
        "cik,cjk->cij",
        lax.all_gather(left_major, "gy", axis=2, tiled=True),
        right_mine,
        preferred_element_type=jnp.float32,
    )
    tri_norm = channel_norm(triangle, out_gain, out_bias).astype(jnp.bfloat16)
    gate = jax.nn.sigmoid(jnp.dot(flat, w_gate, preferred_element_type=jnp.float32)).reshape(
        tile_rows, tile_cols, width
    )
    projected = jnp.einsum("cij,cd->ijd", tri_norm, w_out, preferred_element_type=jnp.float32)
    return (gate * projected).astype(jnp.bfloat16)


def solution(mesh):
    in_specs = (P(("grp", "gx", "gz"), "gy", None), P("grp"), P(), P(), P(), P(), P(), P(), P())
    out_specs = P(("grp", "gx", "gz"), "gy", None)
    return jax.shard_map(body, mesh=mesh, in_specs=in_specs, out_specs=out_specs, check_vma=False)
```

profile of v0, /device:TPU:0, one launch (start us, length us, event | category | flops | bytes accessed | tf_op | source)
XLA Modules:
  0.0 898.8 jit_solution(9406988459465322010)
XLA Ops:
  7.4 3.8 convert_reduce_fusion
  11.2 6.0 fusion.5
  17.2 0.1 broadcast_multiply_fusion
  17.4 4.9 fusion.8
  22.3 13.1 %fusion.25 = f32[128,128,512]{2,1,0:T(8,128)} fusion(bf16[128,128,128]{2,1,0:T(8,128)(2,1)S(1)} %fusion.8, bf16[128,512]{1,0:T(8,128)(2,1)S(1)} %copy-done), kind=kOutput, calls=%fused_computation.34 | convolution fusion | flops 2147483648 | bytes 37879808 | tf_op jit(solution)/shard_map/dot_general | solution.py:28
  35.5 15.6 %fusion.22 = (bf16[128,128,128]{0,2,1:T(8,128)(2,1)}, bf16[128,128,128]{0,2,1:T(8,128)(2,1)}) fusion(f32[128,128,512]{2,1,0:T(8,128)} %fusion.25, f32[128,128]{1,0:T(8,128)S(1)} %broadcast_multiply_fusion), kind=kLoop, calls=%fused_computation.33 | loop fusion | flops 25165824 | bytes 42008576 | tf_op jit(solution)/shard_map/transpose | solution.py:41
  51.1 6.4 copy.13
  57.4 0.0 all-gather.5.cloned.1.call-update
  57.5 0.0 all-gather.3.cloned.1.call-start
  57.5 0.7 all-gather.3.cloned.1.call-update
  58.2 108.0 %all-gather.5.cloned.1.call-done = bf16[128,512,128]{2,0,1:T(8,128)(2,1)} async-done(((bf16[128,128,128]{2,0,1:T(8,128)(2,1)}), bf16[128,512,128]{2,0,1:T(8,128)(2,1)}) %all-gather.5.cloned.1.call-update) | async-done | bytes 16777232 | tf_op jit(solution)/shard_map/all_gather | solution.py:42
  166.2 7.3 all-to-all-start
  173.5 9.0 %fusion.2 = f32[16384,128]{1,0:T(8,128)} fusion(bf16[16384,128]{1,0:T(8,128)(2,1)} %bitcast.24, bf16[128,128]{1,0:T(8,128)(2,1)S(1)} %copy-done.10), kind=kOutput, calls=%fused_computation.3 | convolution fusion | flops 543162368 | bytes 12615680 | tf_op jit(solution)/shard_map/dot_general | solution.py:51
  182.5 580.3 %all-gather.3.cloned.1.call-done = bf16[128,128,512]{0,2,1:T(8,128)(2,1)} async-done(((bf16[128,128,128]{0,2,1:T(8,128)(2,1)}), bf16[128,128,512]{0,2,1:T(8,128)(2,1)}) %all-gather.3.cloned.1.call-update) | async-done | bytes 16777232 | tf_op jit(solution)/shard_map/all_gather | solution.py:46
  762.8 23.4 %copy.15 = bf16[128,128,512]{2,1,0:T(8,128)(2,1)} copy(bf16[128,128,512]{0,2,1:T(8,128)(2,1)} %all-gather.3.cloned.1.call-done) | data formatting | bytes 33554432 | tf_op jit(solution)/shard_map/all_gather | solution.py:46
  786.2 20.3 %all-to-all-done = bf16[128,512,128]{2,0,1:T(8,128)(2,1)} async-done(((bf16[128,512,128]{2,0,1:T(8,128)(2,1)}), bf16[128,512,128]{2,0,1:T(8,128)(2,1)}, u32[]{:S(2)}, u32[]{:S(2)}) %all-to-all-start) | async-done | bytes 16777248 | tf_op jit(solution)/shard_map/all_to_all | solution.py:43
  806.5 22.0 %copy.22 = bf16[128,4,128,128]{3,1,2,0:T(4,128)(2,1)} copy(bf16[128,4,128,128]{3,0,2,1:T(8,128)(2,1)} %bitcast.6) | data formatting | bytes 33554432 | tf_op jit(solution)/shard_map/all_to_all | solution.py:43
  828.6 24.9 %all_to_all.16 = bf16[128,128,512]{2,1,0:T(8,128)(2,1)} reshape(bf16[128,128,4,128]{3,2,1,0:T(4,128)(2,1)} %bitcast.23) | data formatting | bytes 33554432 | tf_op jit(solution)/shard_map/all_to_all | solution.py:43
  853.4 16.4 %fusion.28 = (f32[128,128]{1,0:T(8,128)S(1)}, f32[128,128,128]{2,1,0:T(8,128)}) fusion(bf16[128,128,512]{2,1,0:T(8,128)(2,1)} %copy.15, bf16[128,128,512]{2,1,0:T(8,128)(2,1)} %all_to_all.16), kind=kOutput, calls=%fused_computation.44 | convolution fusion | flops 2149564416 | bytes 42008576 | tf_op jit(solution)/shard_map/cik,cjk->cij/dot_general | solution.py:44
  869.8 4.4 multiply_reduce_fusion
  874.3 1.3 copy-done.2
  875.6 2.0 add_convert_fusion
  877.6 0.0 copy-start.1
  877.6 14.4 %multiply_convert_fusion = bf16[128,128,128]{2,1,0:T(8,128)(2,1)} fusion(f32[128,128,128]{2,1,0:T(8,128)} %bitcast.25, bf16[128,128,128]{2,1,0:T(8,128)(2,1)S(1)} %add_convert_fusion, bf16[128,128]{1,0:T(8,128)(2,1)S(1)} %copy-done.5), kind=kOutput, calls=%fused_computation.27 | convolution fusion | flops 541065216 | bytes 16809984 | tf_op jit(solution)/shard_map/cij,cd->ijd/dot_general | solution.py:54
  (26 shorter events, 0.1 us)
Async XLA Ops:
  6.5 15.8 %copy-start = (bf16[128,512]{1,0:T(8,128)(2,1)S(1)}, bf16[128,512]{1,0:T(8,128)(2,1)}, u32[]{:S(2)}) copy-start(bf16[128,512]{1,0:T(8,128)(2,1)} %param.13) | copy-start | bytes 393220
  6.5 10.8 %copy-start.7 = (f32[128]{0:T(128)S(1)}, f32[128]{0:T(128)}, u32[]{:S(2)}) copy-start(f32[128]{0:T(128)} %param.11) | copy-start | bytes 1540
  6.5 10.8 %copy-start.6 = (f32[128]{0:T(128)S(1)}, f32[128]{0:T(128)}, u32[]{:S(2)}) copy-start(f32[128]{0:T(128)} %param.12) | copy-start | bytes 1540
  6.5 159.7 %all-gather.5.cloned.1.call-start = ((), (), s32[]{:S(2)}) async-start(), calls=%async_computation.2 | async-start | bytes 20971520 | tf_op jit(solution)/shard_map/all_gather | solution.py:42
  6.6 10.8 %copy-start.3 = (bf16[128,128,128]{2,1,0:T(8,128)(2,1)S(1)}, bf16[128,128,128]{2,1,0:T(8,128)(2,1)}, u32[]{:S(2)}) copy-start(bf16[128,128,128]{2,1,0:T(8,128)(2,1)} %param.9) | copy-start | bytes 12582916
  22.3 13.2 %copy-start.4 = (bf16[128,128,128]{2,1,0:T(8,128)(2,1)}, bf16[128,128,128]{2,1,0:T(8,128)(2,1)S(1)}, u32[]{:S(2)}) copy-start(bf16[128,128,128]{2,1,0:T(8,128)(2,1)S(1)} %fusion.8) | copy-start | bytes 12582916
  57.5 705.3 %all-gather.3.cloned.1.call-start = ((), (), s32[]{:S(2)}) async-start(), calls=%async_computation.1 | async-start | bytes 20971520 | tf_op jit(solution)/shard_map/all_gather | solution.py:46
  58.2 115.3 %copy-start.10 = (bf16[128,128]{1,0:T(8,128)(2,1)S(1)}, bf16[128,128]{1,0:T(8,128)(2,1)}, u32[]{:S(2)}) copy-start(bf16[128,128]{1,0:T(8,128)(2,1)} %param.14) | copy-start | bytes 98308
  166.2 640.3 %all-to-all-start = ((bf16[128,512,128]{2,0,1:T(8,128)(2,1)}), bf16[128,512,128]{2,0,1:T(8,128)(2,1)}, u32[]{:S(2)}, u32[]{:S(2)}) async-start(bf16[128,512,128]{2,0,1:T(8,128)(2,1)} %all-gather.5.cloned.1.call-done), calls=%async_computation | async-start | bytes 33554432 | tf_op jit(solution)/shard_map/all_to_all | solution.py:43
  869.8 5.8 copy-start.2
  869.8 5.8 copy-start.8
  869.8 5.8 copy-start.9
  874.2 3.3 copy-start.5
  877.6 14.4 %copy-start.1 = (bf16[128,512]{1,0:T(8,128)(2,1)S(1)}, bf16[128,512]{1,0:T(8,128)(2,1)}, u32[]{:S(2)}) copy-start(bf16[128,512]{1,0:T(8,128)(2,1)} %param.13) | copy-start | bytes 393220
Sparse Core Ops, SparseCore 0:
  57.6 108.6 all-gather.4
  167.8 594.9 all-gather.2
where the time goes:
time: 900 us; the launch traced here: 899 us
  waiting for transfers between devices  709 us (79%)
  local copies, waits for them, and re-layouts  78 us (9%)
  matrix products  52.9 us (6%)
  other arithmetic  36.9 us (4%)
  between operations  14.4 us (2%)
    all_gather x1, waiting for transfers between devices, body(): lax.all_gather(left_major, 'gy', axis=2, tiled=True)  580 us
    all_gather x1, waiting for transfers between devices, body(): column_rows = lax.all_gather(right_major, ('gx', 'gz'), axis=1, tiled=True)  108 us
    all_to_all x2, local copies, waits for them, and re-layouts, body(): lax.all_to_all(column_rows, 'gy', split_axis=1, concat_axis=2, tiled=True)  46.9 us
    all_gather x1, local copies, waits for them, and re-layouts, body(): lax.all_gather(left_major, 'gy', axis=2, tiled=True)  23.4 us
    all_to_all x1, waiting for transfers between devices, body(): lax.all_to_all(column_rows, 'gy', split_axis=1, concat_axis=2, tiled=True)  20.3 us
  transfers between devices with their start and end apart: 3, of which 3 were waited for; matrix products, arithmetic and copies ran while one was open for 4% of the time, Pallas kernels for 0%

commit v1 on v0

--- a/solution.py
+++ b/solution.py
@@ -40,7 +40,10 @@
     left_major = jnp.transpose(left, (2, 0, 1))
     right_major = jnp.transpose(right, (2, 0, 1))
     column_rows = lax.all_gather(right_major, ("gx", "gz"), axis=1, tiled=True)
-    right_mine = lax.all_to_all(column_rows, "gy", split_axis=1, concat_axis=2, tiled=True)
+    right_mine = jnp.concatenate(
+        lax.all_to_all(jnp.stack(jnp.split(column_rows, lax.axis_size("gy"), axis=1)), "gy", 0, 0),
+        axis=2,
+    )
     triangle = jnp.einsum(
         "cik,cjk->cij",
         lax.all_gather(left_major, "gy", axis=2, tiled=True),

time: 900 us -> 863 us (0.959)
  waiting for transfers between devices: 709 us -> 677 us
    all_gather x1, waiting for transfers between devices: 580 us -> 536 us  [body(): lax.all_gather(left_major, 'gy', axis=2, tiled=True)]
    all_to_all x2 -> x1, local copies, waits for them, and re-layouts: 46.9 us -> 14.1 us  [body(): lax.all_to_all(jnp.stack(jnp.split(column_rows, lax.axis_size('gy'), axis...]
    another operation x0 -> x2, local copies, waits for them, and re-layouts: none -> 32 us  [body(): jnp.stack(jnp.split(column_rows, lax.axis_size('gy'), axis=1))]
    all_to_all x1, waiting for transfers between devices: 20.3 us -> 32.7 us  [body(): lax.all_to_all(jnp.stack(jnp.split(column_rows, lax.axis_size('gy'), axis...]
  transfers between devices with their start and end apart: 3 -> 3, of which waited for: 3 -> 3; matrix products, arithmetic and copies ran while one was open for 4% -> 8% of each run, Pallas kernels for 0% -> 0%
where the time goes in v1:
time: 863 us; the launch traced here: 862 us
  waiting for transfers between devices  677 us (78%)
  local copies, waits for them, and re-layouts  76.7 us (9%)
  matrix products  44.5 us (5%)
  other arithmetic  41.3 us (5%)
  between operations  14.4 us (2%)
    all_gather x1, waiting for transfers between devices, body(): lax.all_gather(left_major, 'gy', axis=2, tiled=True)  536 us
    all_gather x1, waiting for transfers between devices, body(): column_rows = lax.all_gather(right_major, ('gx', 'gz'), axis=1, tiled=True)  108 us
    all_to_all x1, waiting for transfers between devices, body(): lax.all_to_all(jnp.stack(jnp.split(column_rows, lax.axis_size('gy'), axis...  32.7 us
    another operation x2, local copies, waits for them, and re-layouts, body(): jnp.stack(jnp.split(column_rows, lax.axis_size('gy'), axis=1))  32 us
    all_gather x1, local copies, waits for them, and re-layouts, body(): lax.all_gather(left_major, 'gy', axis=2, tiled=True)  23.5 us
  transfers between devices with their start and end apart: 3, of which 3 were waited for; matrix products, arithmetic and copies ran while one was open for 8% of the time, Pallas kernels for 0%

profile of v1, /device:TPU:0, one launch (start us, length us, event | category | flops | bytes accessed | tf_op | source)
XLA Modules:
  0.0 861.7 jit_solution(16768042044538117121)
XLA Ops:
  7.4 3.8 convert_reduce_fusion
  11.2 6.0 fusion.5
  17.2 0.1 broadcast_multiply_fusion
  17.4 4.9 fusion.8
  22.3 13.1 %fusion.25 = f32[128,128,512]{2,1,0:T(8,128)} fusion(bf16[128,128,128]{2,1,0:T(8,128)(2,1)S(1)} %fusion.8, bf16[128,512]{1,0:T(8,128)(2,1)S(1)} %copy-done), kind=kOutput, calls=%fused_computation.38 | convolution fusion | flops 2147483648 | bytes 37879808 | tf_op jit(solution)/shard_map/dot_general | solution.py:28
  35.5 15.5 %fusion.22 = (bf16[128,128,128]{0,2,1:T(8,128)(2,1)}, bf16[128,128,128]{0,2,1:T(8,128)(2,1)}) fusion(f32[128,128,512]{2,1,0:T(8,128)} %fusion.25, f32[128,128]{1,0:T(8,128)S(1)} %broadcast_multiply_fusion), kind=kLoop, calls=%fused_computation.37 | loop fusion | flops 25165824 | bytes 42008576 | tf_op jit(solution)/shard_map/transpose | solution.py:41
  51.0 6.4 copy.24
  57.4 0.0 all-gather.3.cloned.1.call-start
  57.5 0.7 all-gather.3.cloned.1.call-update
  58.2 108.0 %all-gather.5.cloned.1.call-done = bf16[128,512,128]{2,0,1:T(8,128)(2,1)} async-done(((bf16[128,128,128]{2,0,1:T(8,128)(2,1)}), bf16[128,512,128]{2,0,1:T(8,128)(2,1)}) %all-gather.5.cloned.1.call-update) | async-done | bytes 16777232 | tf_op jit(solution)/shard_map/all_gather | solution.py:42
  166.2 7.8 slice_bitcast_fusion.3
  174.0 8.0 pad_maximum_fusion
  181.9 24.2 %copy.25 = bf16[4,128,128,128]{2,3,1,0:T(8,128)(2,1)} copy(bf16[4,128,128,128]{3,1,2,0:T(8,128)(2,1)} %pad_maximum_fusion) | data formatting | bytes 33554432 | tf_op jit(solution)/shard_map/stack | solution.py:44
  206.1 7.3 all-to-all-start
  213.4 7.8 fusion.2
  221.2 536.0 %all-gather.3.cloned.1.call-done = bf16[128,128,512]{0,2,1:T(8,128)(2,1)} async-done(((bf16[128,128,128]{0,2,1:T(8,128)(2,1)}), bf16[128,128,512]{0,2,1:T(8,128)(2,1)}) %all-gather.3.cloned.1.call-update) | async-done | bytes 16777232 | tf_op jit(solution)/shard_map/all_gather | solution.py:49
  757.2 23.5 %copy.27 = bf16[128,128,512]{2,1,0:T(8,128)(2,1)} copy(bf16[128,128,512]{0,2,1:T(8,128)(2,1)} %all-gather.3.cloned.1.call-done) | data formatting | bytes 33554432 | tf_op jit(solution)/shard_map/all_gather | solution.py:49
  780.7 32.7 %all-to-all-done = bf16[4,128,128,128]{2,3,1,0:T(8,128)(2,1)} async-done(((bf16[4,128,128,128]{2,3,1,0:T(8,128)(2,1)}), bf16[4,128,128,128]{2,3,1,0:T(8,128)(2,1)}, u32[]{:S(2)}, u32[]{:S(2)}) %all-to-all-start) | async-done | bytes 16777248 | tf_op jit(solution)/shard_map/all_to_all | solution.py:44
  813.4 14.1 %copy.26 = bf16[4,128,128,128]{2,3,0,1:T(8,128)(2,1)} copy(bf16[4,128,128,128]{2,3,1,0:T(8,128)(2,1)} %all-to-all-done) | data formatting | bytes 33554432 | tf_op jit(solution)/shard_map/all_to_all | solution.py:44
  827.5 12.9 %fusion.28 = (f32[128,128]{1,0:T(8,128)S(1)}, f32[128,128,128]{2,1,0:T(8,128)S(1)}) fusion(bf16[128,128,512]{2,1,0:T(8,128)(2,1)} %copy.27, bf16[128,128,512]{1,2,0:T(8,128)(2,1)} %bitcast.30), kind=kOutput, calls=%fused_computation.48 | convolution fusion | flops 2149564416 | bytes 42008576 | tf_op jit(solution)/shard_map/cik,cjk->cij/dot_general | solution.py:47
  840.4 0.9 multiply_reduce_fusion
  841.4 2.0 add_convert_fusion
  843.4 0.7 slice-done.1
  844.1 10.7 %multiply_convert_fusion = bf16[128,128,128]{2,1,0:T(8,128)(2,1)} fusion(f32[128,128,128]{2,1,0:T(8,128)S(1)} %bitcast.34, bf16[128,128,128]{2,1,0:T(8,128)(2,1)S(1)} %add_convert_fusion, bf16[128,128]{1,0:T(8,128)(2,1)S(1)} %copy-done.4), kind=kOutput, calls=%fused_computation.27 | convolution fusion | flops 541065216 | bytes 16809984 | tf_op jit(solution)/shard_map/cij,cd->ijd/dot_general | solution.py:57
  (31 shorter events, 0.1 us)
Async XLA Ops:
  6.5 15.8 %copy-start = (bf16[128,512]{1,0:T(8,128)(2,1)S(1)}, bf16[128,512]{1,0:T(8,128)(2,1)}, u32[]{:S(2)}) copy-start(bf16[128,512]{1,0:T(8,128)(2,1)} %param.13) | copy-start | bytes 393220
  6.5 10.8 %copy-start.6 = (f32[128]{0:T(128)S(1)}, f32[128]{0:T(128)}, u32[]{:S(2)}) copy-start(f32[128]{0:T(128)} %param.11) | copy-start | bytes 1540
  6.5 10.8 %copy-start.5 = (f32[128]{0:T(128)S(1)}, f32[128]{0:T(128)}, u32[]{:S(2)}) copy-start(f32[128]{0:T(128)} %param.12) | copy-start | bytes 1540
  6.5 159.6 %all-gather.5.cloned.1.call-start = ((), (), s32[]{:S(2)}) async-start(), calls=%async_computation.2 | async-start | bytes 20971520 | tf_op jit(solution)/shard_map/all_gather | solution.py:42
  6.6 10.8 %copy-start.2 = (bf16[128,128,128]{2,1,0:T(8,128)(2,1)S(1)}, bf16[128,128,128]{2,1,0:T(8,128)(2,1)}, u32[]{:S(2)}) copy-start(bf16[128,128,128]{2,1,0:T(8,128)(2,1)} %param.9) | copy-start | bytes 12582916
  22.3 13.1 %copy-start.3 = (bf16[128,128,128]{2,1,0:T(8,128)(2,1)}, bf16[128,128,128]{2,1,0:T(8,128)(2,1)S(1)}, u32[]{:S(2)}) copy-start(bf16[128,128,128]{2,1,0:T(8,128)(2,1)S(1)} %fusion.8) | copy-start | bytes 12582916
  57.4 699.8 %all-gather.3.cloned.1.call-start = ((), (), s32[]{:S(2)}) async-start(), calls=%async_computation.1 | async-start | bytes 20971520 | tf_op jit(solution)/shard_map/all_gather | solution.py:49
  206.1 7.3 copy-start.9
  206.1 607.3 %all-to-all-start = ((bf16[4,128,128,128]{2,3,1,0:T(8,128)(2,1)}), bf16[4,128,128,128]{2,3,1,0:T(8,128)(2,1)}, u32[]{:S(2)}, u32[]{:S(2)}) async-start(bf16[4,128,128,128]{2,3,1,0:T(8,128)(2,1)} %copy.25), calls=%async_computation | async-start | bytes 33554432 | tf_op jit(solution)/shard_map/all_to_all | solution.py:44
  840.4 1.0 copy-start.7
  840.4 1.0 copy-start.8
  840.4 3.0 slice-start
  841.3 2.1 copy-start.4
  841.4 2.8 slice-start.1
  843.4 11.4 %copy-start.1 = (bf16[128,512]{1,0:T(8,128)(2,1)S(1)}, bf16[128,512]{1,0:T(8,128)(2,1)}, u32[]{:S(2)}) copy-start(bf16[128,512]{1,0:T(8,128)(2,1)} %param.13) | copy-start | bytes 393220
Sparse Core Ops, SparseCore 0:
  57.5 108.6 all-gather.4
  167.7 589.4 all-gather.2
